TPU v7x, 32 devices: a whole 2x2x4 slice. The times are simulated.
32 devices in a mesh: gx: 8 (over z, core), gy: 4 (over y, x).
Axes of the slice: x: 2, y: 2, z: 4, core: 2. Of those that a mesh axis runs over, the one named last changes fastest.
Arguments:
- velocity: float32 [3, 128, 64, 128], P(None, 'gx', 'gy'), may hold values from -6 to 6
- stresses: float32 [6, 128, 64, 128], P(None, 'gx', 'gy'), may hold values from -6 to 6
- buoyancy: float32 [128, 64, 128], P('gx', 'gy'), may hold values from 0.3 to 0.6
- lame_first: float32 [128, 64, 128], P('gx', 'gy'), may hold values from 0.05 to 0.15
- rigidity: float32 [128, 64, 128], P('gx', 'gy'), may hold values from 0.04 to 0.12
- histories: bfloat16 [8192, 512], P(('gx', 'gy')), may hold values from -6 to 6
- mechanism: bfloat16 [8192, 6], P(('gx', 'gy')), may hold values from -6 to 6
- resample: bfloat16 [512, 3], replicated, may hold values from -0.25 to 0.25
- owners: int32 [8192, 1], P(('gx', 'gy')), may hold values from 0 to 3; in each aligned block of 256 rows (0 to 255, 256 to 511, ...) at most 64 rows name the same one
- cell_offsets: int32 [8192], P(('gx', 'gy')), may hold values from 0 to 32767
Outputs:
- velocity_out: float32 [3, 128, 64, 128], P(None, 'gx', 'gy')
- stresses_out: float32 [6, 128, 64, 128], P(None, 'gx', 'gy')
Inputs may be any that keep to these rules, and one draw needn't show every extreme that they name: `owners`: among the 256 rows of one device at most 64 name the same owner, a bound that some block reaches of them. `cell_offsets`: cell index x * 16 * 128 + y * 128 + z within the enclosing block.
All inputs are finite; a program needn't handle non-finite values.
Results may differ from a plain program's by a relative error of at most 0.00052.
Values may be sent and summed in bfloat16 or wider, within the bound.
A program may use at most 64 MiB of HBM per device.

v0:
```python
import jax
import jax.numpy as jnp
from jax import lax
from jax.sharding import PartitionSpec as P

INNER_WEIGHT = 9.0 / 8.0
OUTER_WEIGHT = -1.0 / 24.0


def extended(cells, sides, width):
    for axis, dim in sides:
        count = lax.axis_size(axis)
        ends = count - 1
        head = lax.slice_in_dim(cells, 0, width, axis=dim)
        tail = lax.slice_in_dim(cells, cells.shape[dim] - width, cells.shape[dim], axis=dim)
        cells = jnp.concatenate(
            [
                lax.ppermute(tail, axis, [(i, (i + 1) % count) for i in range(ends)]),
                cells,
                lax.ppermute(head, axis, [((i + 1) % count, i) for i in range(ends)]),
            ],
            axis=dim,
        )
    return cells


def differ(values, dimension, forward):
    if dimension == 2:
        values = jnp.pad(values, ((0, 0), (0, 0), (2, 2)))
    extent = values.shape[dimension] - 4

    def window(start_at):
        return lax.slice_in_dim(values, start_at, start_at + extent, axis=dimension)

    if forward:
        result = INNER_WEIGHT * (window(3) - window(2)) + OUTER_WEIGHT * (window(4) - window(1))
    else:
        result = INNER_WEIGHT * (window(2) - window(1)) + OUTER_WEIGHT * (window(3) - window(0))
    for second in (0, 1):
        if second != dimension:
            result = lax.slice_in_dim(result, 2, result.shape[second] - 2, axis=second)
    return result


def advance_velocity(velocity, stresses, buoyancy):
    forces = jnp.stack(
        [
            differ(stresses[0], 0, True)
            + differ(stresses[3], 1, False)
            + differ(stresses[4], 2, False),
            differ(stresses[3], 0, False)
            + differ(stresses[1], 1, True)
            + differ(stresses[5], 2, False),
            differ(stresses[4], 0, False)
            + differ(stresses[5], 1, False)
            + differ(stresses[2], 2, True),
        ]
    )
    return velocity + buoyancy * forces


def advance_stress(stresses, velocity, lame_first, rigidity):
    stretch_one = differ(velocity[0], 0, False)
    stretch_two = differ(velocity[1], 1, False)
    stretch_three = differ(velocity[2], 2, False)
    change = stretch_one + stretch_two + stretch_three
    rates = jnp.stack(
        [
            lame_first * change + 2.0 * rigidity * stretch_one,
            lame_first * change + 2.0 * rigidity * stretch_two,
            lame_first * change + 2.0 * rigidity * stretch_three,
            rigidity * (differ(velocity[0], 1, True) + differ(velocity[1], 0, True)),
            rigidity * (differ(velocity[0], 2, True) + differ(velocity[2], 0, True)),
            rigidity * (differ(velocity[1], 2, True) + differ(velocity[2], 1, True)),
        ]
    )
    return stresses + rates


def local(
    velocity,
    stresses,
    buoyancy,
    lame_first,
    rigidity,
    histories,
    mechanism,
    resample,
    owners,
    cell_offsets,
):
    groups = lax.axis_size("gy")
    src_rows = histories.shape[0]
    capacity = src_rows // 4
    across = velocity.shape[1]
    normal = velocity.shape[2]
    levels = velocity.shape[3]
    steps_count = resample.shape[1]
    owner_column = owners[:, 0]
    targets = jnp.arange(groups, dtype=jnp.int32)
    hits = (owner_column[:, None] == targets[None, :]).astype(jnp.int32)
    earlier = jnp.cumsum(hits, axis=0) - hits
    rank_within = jnp.sum(earlier * hits, axis=1)
    slots = owner_column * capacity + rank_within
    cell_buffer = (
        jnp.zeros((groups * capacity,), jnp.int32)
        .at[slots]
        .set(cell_offsets)
        .reshape(groups, capacity)
    )
    arrived_cells = lax.all_to_all(cell_buffer, "gy", split_axis=0, concat_axis=0, tiled=True)
    amplitude = jnp.dot(histories, resample, preferred_element_type=jnp.float32)
    local_terms = (mechanism.astype(jnp.float32)[:, :, None] * amplitude[:, None, :]).astype(
        jnp.bfloat16
    )
    local_terms = local_terms.reshape(src_rows, -1)
    term_buffer = (
        jnp.zeros((groups * capacity, local_terms.shape[1]), jnp.bfloat16)
        .at[slots]
        .set(local_terms)
    )
    arrived = lax.all_to_all(
        term_buffer.reshape(groups, capacity, -1), "gy", split_axis=0, concat_axis=0, tiled=True
    )
    slot_count = groups * capacity
    flat_terms = arrived.reshape(slot_count, 6, steps_count)
    flat_cells = arrived_cells.reshape(slot_count)
    plane = flat_cells // levels
    height = flat_cells % levels
    pick_plane = (plane[:, None] == jnp.arange(across * normal, dtype=jnp.int32)[None, :]).astype(
        jnp.bfloat16
    )
    pick_level = (height[:, None] == jnp.arange(levels, dtype=jnp.int32)[None, :]).astype(
        jnp.bfloat16
    )
    spread = (flat_terms[:, :, :, None] * pick_level[:, None, None, :]).reshape(slot_count, -1)
    placed = jnp.einsum("rp,rk->pk", pick_plane, spread, preferred_element_type=jnp.float32)
    placed = placed.reshape(across, normal, 6, steps_count, levels).transpose(3, 2, 0, 1, 4)
    for step_index in range(steps_count):
        padded_stress = extended(stresses, (("gx", 1), ("gy", 2)), 2)
        velocity = advance_velocity(velocity, padded_stress, buoyancy)
        padded_velocity = extended(velocity, (("gx", 1), ("gy", 2)), 2)
        stresses = advance_stress(stresses, padded_velocity, lame_first, rigidity)
        stresses = stresses + placed[step_index]
    return (velocity, stresses)


def solution(mesh):
    in_specs = (
        P(None, "gx", "gy", None),
        P(None, "gx", "gy", None),
        P("gx", "gy", None),
        P("gx", "gy", None),
        P("gx", "gy", None),
        P(("gx", "gy"), None),
        P(("gx", "gy"), None),
        P(),
        P(("gx", "gy"), None),
        P(("gx", "gy")),
    )
    out_specs = (P(None, "gx", "gy", None), P(None, "gx", "gy", None))
    return jax.shard_map(local, mesh=mesh, in_specs=in_specs, out_specs=out_specs, check_vma=False)
```

profile of v0, /device:TPU:0, one launch (start us, length us, event | category | flops | bytes accessed | tf_op | source)
XLA Modules:
  0.0 137.4 jit_solution(13856748849556186472)
XLA Ops:
  0.7 1.0 fusion.269
  1.7 2.4 %collective-permute-start = (f32[6,2,16,128]{3,2,1,0:T(8,128)S(1)}, f32[6,2,16,128]{3,2,1,0:T(8,128)S(1)}, u32[]{:S(2)}, u32[]{:S(2)}) collective-permute-start(f32[6,2,16,128]{3,2,1,0:T(8,128)S(1)} %get-tuple-element.59), channel_id=1, source_target_pairs={{0,4},{4,8},{8,12},{12,16},{16,20},{20,24},{24,28},{1,5},{5,9},{9,... | collective-permute-start | bytes 294920 | tf_op jit(solution)/shard_map/ppermute | solution.py:18
  4.1 1.3 collective-permute-start.1
  5.4 0.7 compare_convert_fusion
  6.1 1.2 reduce-window.6
  7.7 0.7 fusion.256
  8.4 0.7 compare_select_fusion
  9.1 1.6 %scatter_custom_fusion = s32[256]{0:T(256)S(1)} fusion(s32[256]{0:T(256)S(1)} %bitcast.233, s32[256]{0:T(256)} %param.19, s32[]{:T(128)} %constant.44.clone.1), kind=kCustom, calls=%fused_computation.510 | custom fusion | bytes 1536 | tf_op jit(solution)/shard_map/scatter | solution.py:108
  10.6 0.7 all_to_all.9
  11.3 4.5 %all-to-all-start = ((s32[4,1,64]{2,1,0:T(1,128)}), s32[4,1,64]{2,1,0:T(1,128)S(1)}, u32[]{:S(2)}, u32[]{:S(2)}) async-start(s32[4,1,64]{2,1,0:T(1,128)} %all_to_all.9), calls=%async_computation | async-start | bytes 4096 | tf_op jit(solution)/shard_map/all_to_all | solution.py:111
  15.8 0.7 convert_element_type.46
  16.5 0.8 fusion.291
  17.6 1.2 scatter_custom_fusion.1
  18.9 0.7 reshape.364
  19.6 0.8 all-to-all-done
  20.4 3.3 %all-to-all-start.1 = ((bf16[4,2,576]{2,1,0:T(2,128)(2,1)}), bf16[4,2,576]{2,1,0:T(2,128)(2,1)S(1)}, u32[]{:S(2)}, u32[]{:S(2)}) async-start(bf16[4,2,576]{2,1,0:T(2,128)(2,1)} %reshape.364), calls=%async_computation.1 | async-start | bytes 20480 | tf_op jit(solution)/shard_map/all_to_all | solution.py:122
  23.8 0.5 broadcast.418
  24.3 0.7 reduce.3
  25.3 3.9 %collective-permute-start.2 = (f32[6,20,2,128]{3,2,1,0:T(2,128)S(1)}, f32[6,20,2,128]{3,2,1,0:T(2,128)S(1)}, u32[]{:S(2)}, u32[]{:S(2)}) collective-permute-start(f32[6,20,2,128]{3,2,1,0:T(2,128)S(1)} %get-tuple-element.52), channel_id=1, source_target_pairs={{0,1},{1,2},{2,3},{4,5},{5,6},{6,7},{8,9},{9,10},{10,11},{12,13},{... | collective-permute-start | bytes 368648 | tf_op jit(solution)/shard_map/ppermute | solution.py:18
  29.2 1.3 collective-permute-start.3
  30.8 1.8 %collective-permute-done.2 = f32[6,20,2,128]{3,2,1,0:T(2,128)S(1)} collective-permute-done((f32[6,20,2,128]{3,2,1,0:T(2,128)S(1)}, f32[6,20,2,128]{3,2,1,0:T(2,128)S(1)}, u32[]{:S(2)}, u32[]{:S(2)}) %collective-permute-start.2) | collective-permute-done | bytes 122912 | tf_op jit(solution)/shard_map/ppermute | solution.py:18
  32.5 4.8 %collective-permute-done.3 = f32[6,20,2,128]{3,2,1,0:T(2,128)S(1)} collective-permute-done((f32[6,20,2,128]{3,2,1,0:T(2,128)S(1)}, f32[6,20,2,128]{3,2,1,0:T(2,128)S(1)}, u32[]{:S(2)}, u32[]{:S(2)}) %collective-permute-start.3) | collective-permute-done | bytes 122912 | tf_op jit(solution)/shard_map/ppermute | solution.py:20
  37.8 0.4 pad_slice_fusion.47
  38.2 0.3 pad_slice_fusion.53
  39.0 0.8 copy-done.4
  39.8 2.0 %collective-permute-start.4 = (f32[3,2,16,128]{3,2,1,0:T(8,128)S(1)}, f32[3,2,16,128]{3,2,1,0:T(8,128)S(1)}, u32[]{:S(2)}, u32[]{:S(2)}) collective-permute-start(f32[3,2,16,128]{3,2,1,0:T(8,128)S(1)} %get-tuple-element.88), channel_id=1, source_target_pairs={{0,4},{4,8},{8,12},{12,16},{16,20},{20,24},{24,28},{1,5},{5,9},{9,... | collective-permute-start | bytes 147464 | tf_op jit(solution)/shard_map/ppermute | solution.py:18
  41.9 1.3 collective-permute-start.5
  43.2 0.5 convolution_bitcast_fusion
  43.7 3.7 %collective-permute-done.5 = f32[3,2,16,128]{3,2,1,0:T(8,128)S(1)} collective-permute-done((f32[3,2,16,128]{3,2,1,0:T(8,128)S(1)}, f32[3,2,16,128]{3,2,1,0:T(8,128)S(1)}, u32[]{:S(2)}, u32[]{:S(2)}) %collective-permute-start.5) | collective-permute-done | bytes 49184 | tf_op jit(solution)/shard_map/ppermute | solution.py:20
  47.5 4.1 %collective-permute-start.6 = (f32[3,20,2,128]{3,2,1,0:T(2,128)S(1)}, f32[3,20,2,128]{3,2,1,0:T(2,128)S(1)}, u32[]{:S(2)}, u32[]{:S(2)}) collective-permute-start(f32[3,20,2,128]{3,2,1,0:T(2,128)S(1)} %get-tuple-element.82), channel_id=1, source_target_pairs={{0,1},{1,2},{2,3},{4,5},{5,6},{6,7},{8,9},{9,10},{10,11},{12,13},{... | collective-permute-start | bytes 184328 | tf_op jit(solution)/shard_map/ppermute | solution.py:18
  51.6 1.3 collective-permute-start.7
  53.0 0.4 collective-permute-done.6
  53.5 4.3 %collective-permute-done.7 = f32[3,20,2,128]{3,2,1,0:T(2,128)S(1)} collective-permute-done((f32[3,20,2,128]{3,2,1,0:T(2,128)S(1)}, f32[3,20,2,128]{3,2,1,0:T(2,128)S(1)}, u32[]{:S(2)}, u32[]{:S(2)}) %collective-permute-start.7) | collective-permute-done | bytes 61472 | tf_op jit(solution)/shard_map/ppermute | solution.py:20
  59.0 0.3 copy-done.1
  60.0 3.3 %collective-permute-start.8 = (f32[6,2,16,128]{3,2,1,0:T(8,128)S(1)}, f32[6,2,16,128]{3,2,1,0:T(8,128)S(1)}, u32[]{:S(2)}, u32[]{:S(2)}) collective-permute-start(f32[6,2,16,128]{3,2,1,0:T(8,128)S(1)} %get-tuple-element.56), channel_id=1, source_target_pairs={{0,4},{4,8},{8,12},{12,16},{16,20},{20,24},{24,28},{1,5},{5,9},{9,... | collective-permute-start | bytes 294920 | tf_op jit(solution)/shard_map/ppermute | solution.py:18
  63.3 1.3 collective-permute-start.9
  64.6 3.0 %collective-permute-done.9 = f32[6,2,16,128]{3,2,1,0:T(8,128)S(1)} collective-permute-done((f32[6,2,16,128]{3,2,1,0:T(8,128)S(1)}, f32[6,2,16,128]{3,2,1,0:T(8,128)S(1)}, u32[]{:S(2)}, u32[]{:S(2)}) %collective-permute-start.9) | collective-permute-done | bytes 98336 | tf_op jit(solution)/shard_map/ppermute | solution.py:20
  67.7 3.4 %collective-permute-start.10 = (f32[6,20,2,128]{3,2,1,0:T(2,128)S(1)}, f32[6,20,2,128]{3,2,1,0:T(2,128)S(1)}, u32[]{:S(2)}, u32[]{:S(2)}) collective-permute-start(f32[6,20,2,128]{3,2,1,0:T(2,128)S(1)} %get-tuple-element.50), channel_id=1, source_target_pairs={{0,1},{1,2},{2,3},{4,5},{5,6},{6,7},{8,9},{9,10},{10,11},{12,13},{... | collective-permute-start | bytes 368648 | tf_op jit(solution)/shard_map/ppermute | solution.py:18
  71.1 1.3 collective-permute-start.11
  72.4 1.1 collective-permute-done.10
  73.5 4.4 %collective-permute-done.11 = f32[6,20,2,128]{3,2,1,0:T(2,128)S(1)} collective-permute-done((f32[6,20,2,128]{3,2,1,0:T(2,128)S(1)}, f32[6,20,2,128]{3,2,1,0:T(2,128)S(1)}, u32[]{:S(2)}, u32[]{:S(2)}) %collective-permute-start.11) | collective-permute-done | bytes 122912 | tf_op jit(solution)/shard_map/ppermute | solution.py:20
  79.8 3.7 %collective-permute-start.12 = (f32[3,2,16,128]{3,2,1,0:T(8,128)S(1)}, f32[3,2,16,128]{3,2,1,0:T(8,128)S(1)}, u32[]{:S(2)}, u32[]{:S(2)}) collective-permute-start(f32[3,2,16,128]{3,2,1,0:T(8,128)S(1)} %get-tuple-element.86), channel_id=1, source_target_pairs={{0,4},{4,8},{8,12},{12,16},{16,20},{20,24},{24,28},{1,5},{5,9},{9,... | collective-permute-start | bytes 147464 | tf_op jit(solution)/shard_map/ppermute | solution.py:18
  83.5 1.3 collective-permute-start.13
  84.8 3.5 %collective-permute-done.13 = f32[3,2,16,128]{3,2,1,0:T(8,128)S(1)} collective-permute-done((f32[3,2,16,128]{3,2,1,0:T(8,128)S(1)}, f32[3,2,16,128]{3,2,1,0:T(8,128)S(1)}, u32[]{:S(2)}, u32[]{:S(2)}) %collective-permute-start.13) | collective-permute-done | bytes 49184 | tf_op jit(solution)/shard_map/ppermute | solution.py:20
  88.3 2.5 %collective-permute-start.14 = (f32[3,20,2,128]{3,2,1,0:T(2,128)S(1)}, f32[3,20,2,128]{3,2,1,0:T(2,128)S(1)}, u32[]{:S(2)}, u32[]{:S(2)}) collective-permute-start(f32[3,20,2,128]{3,2,1,0:T(2,128)S(1)} %get-tuple-element.80), channel_id=1, source_target_pairs={{0,1},{1,2},{2,3},{4,5},{5,6},{6,7},{8,9},{9,10},{10,11},{12,13},{... | collective-permute-start | bytes 184328 | tf_op jit(solution)/shard_map/ppermute | solution.py:18
  90.8 1.3 collective-permute-start.15
  92.1 0.5 collective-permute-done.14
  92.7 4.3 %collective-permute-done.15 = f32[3,20,2,128]{3,2,1,0:T(2,128)S(1)} collective-permute-done((f32[3,20,2,128]{3,2,1,0:T(2,128)S(1)}, f32[3,20,2,128]{3,2,1,0:T(2,128)S(1)}, u32[]{:S(2)}, u32[]{:S(2)}) %collective-permute-start.15) | collective-permute-done | bytes 61472 | tf_op jit(solution)/shard_map/ppermute | solution.py:20
  97.9 0.3 pad_slice_fusion.26
  98.9 3.3 %collective-permute-start.16 = (f32[6,2,16,128]{3,2,1,0:T(8,128)S(1)}, f32[6,2,16,128]{3,2,1,0:T(8,128)S(1)}, u32[]{:S(2)}, u32[]{:S(2)}) collective-permute-start(f32[6,2,16,128]{3,2,1,0:T(8,128)S(1)} %get-tuple-element.54), channel_id=1, source_target_pairs={{0,4},{4,8},{8,12},{12,16},{16,20},{20,24},{24,28},{1,5},{5,9},{9,... | collective-permute-start | bytes 294920 | tf_op jit(solution)/shard_map/ppermute | solution.py:18
  102.1 1.3 collective-permute-start.17
  103.4 2.8 %collective-permute-done.17 = f32[6,2,16,128]{3,2,1,0:T(8,128)S(1)} collective-permute-done((f32[6,2,16,128]{3,2,1,0:T(8,128)S(1)}, f32[6,2,16,128]{3,2,1,0:T(8,128)S(1)}, u32[]{:S(2)}, u32[]{:S(2)}) %collective-permute-start.17) | collective-permute-done | bytes 98336 | tf_op jit(solution)/shard_map/ppermute | solution.py:20
  106.3 2.8 %collective-permute-start.18 = (f32[6,20,2,128]{3,2,1,0:T(2,128)S(1)}, f32[6,20,2,128]{3,2,1,0:T(2,128)S(1)}, u32[]{:S(2)}, u32[]{:S(2)}) collective-permute-start(f32[6,20,2,128]{3,2,1,0:T(2,128)S(1)} %get-tuple-element.48), channel_id=1, source_target_pairs={{0,1},{1,2},{2,3},{4,5},{5,6},{6,7},{8,9},{9,10},{10,11},{12,13},{... | collective-permute-start | bytes 368648 | tf_op jit(solution)/shard_map/ppermute | solution.py:18
  109.2 1.5 %collective-permute-start.19 = (f32[6,20,2,128]{3,2,1,0:T(2,128)S(1)}, f32[6,20,2,128]{3,2,1,0:T(2,128)S(1)}, u32[]{:S(2)}, u32[]{:S(2)}) collective-permute-start(f32[6,20,2,128]{3,2,1,0:T(2,128)S(1)} %get-tuple-element.49), channel_id=1, source_target_pairs={{1,0},{2,1},{3,2},{5,4},{6,5},{7,6},{9,8},{10,9},{11,10},{13,12},{... | collective-permute-start | bytes 368648 | tf_op jit(solution)/shard_map/ppermute | solution.py:20
  110.6 0.9 collective-permute-done.18
  111.6 4.4 %collective-permute-done.19 = f32[6,20,2,128]{3,2,1,0:T(2,128)S(1)} collective-permute-done((f32[6,20,2,128]{3,2,1,0:T(2,128)S(1)}, f32[6,20,2,128]{3,2,1,0:T(2,128)S(1)}, u32[]{:S(2)}, u32[]{:S(2)}) %collective-permute-start.19) | collective-permute-done | bytes 122912 | tf_op jit(solution)/shard_map/ppermute | solution.py:20
  117.9 3.7 %collective-permute-start.20 = (f32[3,2,16,128]{3,2,1,0:T(8,128)S(1)}, f32[3,2,16,128]{3,2,1,0:T(8,128)S(1)}, u32[]{:S(2)}, u32[]{:S(2)}) collective-permute-start(f32[3,2,16,128]{3,2,1,0:T(8,128)S(1)} %get-tuple-element.84), channel_id=1, source_target_pairs={{0,4},{4,8},{8,12},{12,16},{16,20},{20,24},{24,28},{1,5},{5,9},{9,... | collective-permute-start | bytes 147464 | tf_op jit(solution)/shard_map/ppermute | solution.py:18
  121.6 1.3 collective-permute-start.21
  122.9 2.8 %collective-permute-done.21 = f32[3,2,16,128]{3,2,1,0:T(8,128)S(1)} collective-permute-done((f32[3,2,16,128]{3,2,1,0:T(8,128)S(1)}, f32[3,2,16,128]{3,2,1,0:T(8,128)S(1)}, u32[]{:S(2)}, u32[]{:S(2)}) %collective-permute-start.21) | collective-permute-done | bytes 49184 | tf_op jit(solution)/shard_map/ppermute | solution.py:20
  125.7 2.7 %collective-permute-start.22 = (f32[3,20,2,128]{3,2,1,0:T(2,128)S(1)}, f32[3,20,2,128]{3,2,1,0:T(2,128)S(1)}, u32[]{:S(2)}, u32[]{:S(2)}) collective-permute-start(f32[3,20,2,128]{3,2,1,0:T(2,128)S(1)} %get-tuple-element.78), channel_id=1, source_target_pairs={{0,1},{1,2},{2,3},{4,5},{5,6},{6,7},{8,9},{9,10},{10,11},{12,13},{... | collective-permute-start | bytes 184328 | tf_op jit(solution)/shard_map/ppermute | solution.py:18
  128.4 1.3 collective-permute-start.23
  129.7 0.5 collective-permute-done.22
  130.3 4.3 %collective-permute-done.23 = f32[3,20,2,128]{3,2,1,0:T(2,128)S(1)} collective-permute-done((f32[3,20,2,128]{3,2,1,0:T(2,128)S(1)}, f32[3,20,2,128]{3,2,1,0:T(2,128)S(1)}, u32[]{:S(2)}, u32[]{:S(2)}) %collective-permute-start.23) | collective-permute-done | bytes 61472 | tf_op jit(solution)/shard_map/ppermute | solution.py:20
  136.5 0.9 copy.63
  (134 shorter events, 11.6 us)
Async XLA Ops:
  0.6 15.9 %copy-start = (bf16[256,512]{1,0:T(8,128)(2,1)S(1)}, bf16[256,512]{1,0:T(8,128)(2,1)}, u32[]{:S(2)}) copy-start(bf16[256,512]{1,0:T(8,128)(2,1)} %param.15) | copy-start | bytes 786436
  0.6 24.4 %copy-start.3 = (f32[6,16,16,128]{3,2,1,0:T(8,128)S(1)}, f32[6,16,16,128]{3,2,1,0:T(8,128)}, u32[]{:S(2)}) copy-start(f32[6,16,16,128]{3,2,1,0:T(8,128)} %param.11) | copy-start | bytes 2359300
  1.7 23.4 %collective-permute-start = (f32[6,2,16,128]{3,2,1,0:T(8,128)S(1)}, f32[6,2,16,128]{3,2,1,0:T(8,128)S(1)}, u32[]{:S(2)}, u32[]{:S(2)}) collective-permute-start(f32[6,2,16,128]{3,2,1,0:T(8,128)S(1)} %get-tuple-element.59), channel_id=1, source_target_pairs={{0,4},{4,8},{8,12},{12,16},{16,20},{20,24},{24,28},{1,5},{5,9},{9,... | collective-permute-start | bytes 294920 | tf_op jit(solution)/shard_map/ppermute | solution.py:18
  4.1 21.0 %collective-permute-start.1 = (f32[6,2,16,128]{3,2,1,0:T(8,128)S(1)}, f32[6,2,16,128]{3,2,1,0:T(8,128)S(1)}, u32[]{:S(2)}, u32[]{:S(2)}) collective-permute-start(f32[6,2,16,128]{3,2,1,0:T(8,128)S(1)} %get-tuple-element.58), channel_id=1, source_target_pairs={{4,0},{8,4},{12,8},{16,12},{20,16},{24,20},{28,24},{5,1},{9,5},{13... | collective-permute-start | bytes 294920 | tf_op jit(solution)/shard_map/ppermute | solution.py:20
  11.3 9.1 %all-to-all-start = ((s32[4,1,64]{2,1,0:T(1,128)}), s32[4,1,64]{2,1,0:T(1,128)S(1)}, u32[]{:S(2)}, u32[]{:S(2)}) async-start(s32[4,1,64]{2,1,0:T(1,128)} %all_to_all.9), calls=%async_computation | async-start | bytes 4096 | tf_op jit(solution)/shard_map/all_to_all | solution.py:111
  20.4 10.1 %all-to-all-start.1 = ((bf16[4,2,576]{2,1,0:T(2,128)(2,1)}), bf16[4,2,576]{2,1,0:T(2,128)(2,1)S(1)}, u32[]{:S(2)}, u32[]{:S(2)}) async-start(bf16[4,2,576]{2,1,0:T(2,128)(2,1)} %reshape.364), calls=%async_computation.1 | async-start | bytes 20480 | tf_op jit(solution)/shard_map/all_to_all | solution.py:122
  25.3 7.2 %collective-permute-start.2 = (f32[6,20,2,128]{3,2,1,0:T(2,128)S(1)}, f32[6,20,2,128]{3,2,1,0:T(2,128)S(1)}, u32[]{:S(2)}, u32[]{:S(2)}) collective-permute-start(f32[6,20,2,128]{3,2,1,0:T(2,128)S(1)} %get-tuple-element.52), channel_id=1, source_target_pairs={{0,1},{1,2},{2,3},{4,5},{5,6},{6,7},{8,9},{9,10},{10,11},{12,13},{... | collective-permute-start | bytes 368648 | tf_op jit(solution)/shard_map/ppermute | solution.py:18
  29.2 8.1 %collective-permute-start.3 = (f32[6,20,2,128]{3,2,1,0:T(2,128)S(1)}, f32[6,20,2,128]{3,2,1,0:T(2,128)S(1)}, u32[]{:S(2)}, u32[]{:S(2)}) collective-permute-start(f32[6,20,2,128]{3,2,1,0:T(2,128)S(1)} %get-tuple-element.53), channel_id=1, source_target_pairs={{1,0},{2,1},{3,2},{5,4},{6,5},{7,6},{9,8},{10,9},{11,10},{13,12},{... | collective-permute-start | bytes 368648 | tf_op jit(solution)/shard_map/ppermute | solution.py:20
  38.7 1.0 copy-start.4
  38.7 1.0 copy-start.5
  39.8 3.9 %collective-permute-start.4 = (f32[3,2,16,128]{3,2,1,0:T(8,128)S(1)}, f32[3,2,16,128]{3,2,1,0:T(8,128)S(1)}, u32[]{:S(2)}, u32[]{:S(2)}) collective-permute-start(f32[3,2,16,128]{3,2,1,0:T(8,128)S(1)} %get-tuple-element.88), channel_id=1, source_target_pairs={{0,4},{4,8},{8,12},{12,16},{16,20},{20,24},{24,28},{1,5},{5,9},{9,... | collective-permute-start | bytes 147464 | tf_op jit(solution)/shard_map/ppermute | solution.py:18
  41.9 5.6 %collective-permute-start.5 = (f32[3,2,16,128]{3,2,1,0:T(8,128)S(1)}, f32[3,2,16,128]{3,2,1,0:T(8,128)S(1)}, u32[]{:S(2)}, u32[]{:S(2)}) collective-permute-start(f32[3,2,16,128]{3,2,1,0:T(8,128)S(1)} %get-tuple-element.89), channel_id=1, source_target_pairs={{4,0},{8,4},{12,8},{16,12},{20,16},{24,20},{28,24},{5,1},{9,5},{13... | collective-permute-start | bytes 147464 | tf_op jit(solution)/shard_map/ppermute | solution.py:20
  47.5 6.0 %collective-permute-start.6 = (f32[3,20,2,128]{3,2,1,0:T(2,128)S(1)}, f32[3,20,2,128]{3,2,1,0:T(2,128)S(1)}, u32[]{:S(2)}, u32[]{:S(2)}) collective-permute-start(f32[3,20,2,128]{3,2,1,0:T(2,128)S(1)} %get-tuple-element.82), channel_id=1, source_target_pairs={{0,1},{1,2},{2,3},{4,5},{5,6},{6,7},{8,9},{9,10},{10,11},{12,13},{... | collective-permute-start | bytes 184328 | tf_op jit(solution)/shard_map/ppermute | solution.py:18
  51.6 6.1 %collective-permute-start.7 = (f32[3,20,2,128]{3,2,1,0:T(2,128)S(1)}, f32[3,20,2,128]{3,2,1,0:T(2,128)S(1)}, u32[]{:S(2)}, u32[]{:S(2)}) collective-permute-start(f32[3,20,2,128]{3,2,1,0:T(2,128)S(1)} %get-tuple-element.83), channel_id=1, source_target_pairs={{1,0},{2,1},{3,2},{5,4},{6,5},{7,6},{9,8},{10,9},{11,10},{13,12},{... | collective-permute-start | bytes 184328 | tf_op jit(solution)/shard_map/ppermute | solution.py:20
  58.4 0.9 copy-start.1
  58.4 1.0 copy-start.6
  60.0 4.6 %collective-permute-start.8 = (f32[6,2,16,128]{3,2,1,0:T(8,128)S(1)}, f32[6,2,16,128]{3,2,1,0:T(8,128)S(1)}, u32[]{:S(2)}, u32[]{:S(2)}) collective-permute-start(f32[6,2,16,128]{3,2,1,0:T(8,128)S(1)} %get-tuple-element.56), channel_id=1, source_target_pairs={{0,4},{4,8},{8,12},{12,16},{16,20},{20,24},{24,28},{1,5},{5,9},{9,... | collective-permute-start | bytes 294920 | tf_op jit(solution)/shard_map/ppermute | solution.py:18
  63.3 4.3 %collective-permute-start.9 = (f32[6,2,16,128]{3,2,1,0:T(8,128)S(1)}, f32[6,2,16,128]{3,2,1,0:T(8,128)S(1)}, u32[]{:S(2)}, u32[]{:S(2)}) collective-permute-start(f32[6,2,16,128]{3,2,1,0:T(8,128)S(1)} %get-tuple-element.57), channel_id=1, source_target_pairs={{4,0},{8,4},{12,8},{16,12},{20,16},{24,20},{28,24},{5,1},{9,5},{13... | collective-permute-start | bytes 294920 | tf_op jit(solution)/shard_map/ppermute | solution.py:20
  67.7 5.8 %collective-permute-start.10 = (f32[6,20,2,128]{3,2,1,0:T(2,128)S(1)}, f32[6,20,2,128]{3,2,1,0:T(2,128)S(1)}, u32[]{:S(2)}, u32[]{:S(2)}) collective-permute-start(f32[6,20,2,128]{3,2,1,0:T(2,128)S(1)} %get-tuple-element.50), channel_id=1, source_target_pairs={{0,1},{1,2},{2,3},{4,5},{5,6},{6,7},{8,9},{9,10},{10,11},{12,13},{... | collective-permute-start | bytes 368648 | tf_op jit(solution)/shard_map/ppermute | solution.py:18
  71.1 6.8 %collective-permute-start.11 = (f32[6,20,2,128]{3,2,1,0:T(2,128)S(1)}, f32[6,20,2,128]{3,2,1,0:T(2,128)S(1)}, u32[]{:S(2)}, u32[]{:S(2)}) collective-permute-start(f32[6,20,2,128]{3,2,1,0:T(2,128)S(1)} %get-tuple-element.51), channel_id=1, source_target_pairs={{1,0},{2,1},{3,2},{5,4},{6,5},{7,6},{9,8},{10,9},{11,10},{13,12},{... | collective-permute-start | bytes 368648 | tf_op jit(solution)/shard_map/ppermute | solution.py:20
  79.8 5.0 %collective-permute-start.12 = (f32[3,2,16,128]{3,2,1,0:T(8,128)S(1)}, f32[3,2,16,128]{3,2,1,0:T(8,128)S(1)}, u32[]{:S(2)}, u32[]{:S(2)}) collective-permute-start(f32[3,2,16,128]{3,2,1,0:T(8,128)S(1)} %get-tuple-element.86), channel_id=1, source_target_pairs={{0,4},{4,8},{8,12},{12,16},{16,20},{20,24},{24,28},{1,5},{5,9},{9,... | collective-permute-start | bytes 147464 | tf_op jit(solution)/shard_map/ppermute | solution.py:18
  83.5 4.8 %collective-permute-start.13 = (f32[3,2,16,128]{3,2,1,0:T(8,128)S(1)}, f32[3,2,16,128]{3,2,1,0:T(8,128)S(1)}, u32[]{:S(2)}, u32[]{:S(2)}) collective-permute-start(f32[3,2,16,128]{3,2,1,0:T(8,128)S(1)} %get-tuple-element.87), channel_id=1, source_target_pairs={{4,0},{8,4},{12,8},{16,12},{20,16},{24,20},{28,24},{5,1},{9,5},{13... | collective-permute-start | bytes 147464 | tf_op jit(solution)/shard_map/ppermute | solution.py:20
  88.3 4.4 %collective-permute-start.14 = (f32[3,20,2,128]{3,2,1,0:T(2,128)S(1)}, f32[3,20,2,128]{3,2,1,0:T(2,128)S(1)}, u32[]{:S(2)}, u32[]{:S(2)}) collective-permute-start(f32[3,20,2,128]{3,2,1,0:T(2,128)S(1)} %get-tuple-element.80), channel_id=1, source_target_pairs={{0,1},{1,2},{2,3},{4,5},{5,6},{6,7},{8,9},{9,10},{10,11},{12,13},{... | collective-permute-start | bytes 184328 | tf_op jit(solution)/shard_map/ppermute | solution.py:18
  90.8 6.1 %collective-permute-start.15 = (f32[3,20,2,128]{3,2,1,0:T(2,128)S(1)}, f32[3,20,2,128]{3,2,1,0:T(2,128)S(1)}, u32[]{:S(2)}, u32[]{:S(2)}) collective-permute-start(f32[3,20,2,128]{3,2,1,0:T(2,128)S(1)} %get-tuple-element.81), channel_id=1, source_target_pairs={{1,0},{2,1},{3,2},{5,4},{6,5},{7,6},{9,8},{10,9},{11,10},{13,12},{... | collective-permute-start | bytes 184328 | tf_op jit(solution)/shard_map/ppermute | solution.py:20
  98.9 4.6 %collective-permute-start.16 = (f32[6,2,16,128]{3,2,1,0:T(8,128)S(1)}, f32[6,2,16,128]{3,2,1,0:T(8,128)S(1)}, u32[]{:S(2)}, u32[]{:S(2)}) collective-permute-start(f32[6,2,16,128]{3,2,1,0:T(8,128)S(1)} %get-tuple-element.54), channel_id=1, source_target_pairs={{0,4},{4,8},{8,12},{12,16},{16,20},{20,24},{24,28},{1,5},{5,9},{9,... | collective-permute-start | bytes 294920 | tf_op jit(solution)/shard_map/ppermute | solution.py:18
  102.1 4.1 %collective-permute-start.17 = (f32[6,2,16,128]{3,2,1,0:T(8,128)S(1)}, f32[6,2,16,128]{3,2,1,0:T(8,128)S(1)}, u32[]{:S(2)}, u32[]{:S(2)}) collective-permute-start(f32[6,2,16,128]{3,2,1,0:T(8,128)S(1)} %get-tuple-element.55), channel_id=1, source_target_pairs={{4,0},{8,4},{12,8},{16,12},{20,16},{24,20},{28,24},{5,1},{9,5},{13... | collective-permute-start | bytes 294920 | tf_op jit(solution)/shard_map/ppermute | solution.py:20
  106.3 5.3 %collective-permute-start.18 = (f32[6,20,2,128]{3,2,1,0:T(2,128)S(1)}, f32[6,20,2,128]{3,2,1,0:T(2,128)S(1)}, u32[]{:S(2)}, u32[]{:S(2)}) collective-permute-start(f32[6,20,2,128]{3,2,1,0:T(2,128)S(1)} %get-tuple-element.48), channel_id=1, source_target_pairs={{0,1},{1,2},{2,3},{4,5},{5,6},{6,7},{8,9},{9,10},{10,11},{12,13},{... | collective-permute-start | bytes 368648 | tf_op jit(solution)/shard_map/ppermute | solution.py:18
  109.2 6.8 %collective-permute-start.19 = (f32[6,20,2,128]{3,2,1,0:T(2,128)S(1)}, f32[6,20,2,128]{3,2,1,0:T(2,128)S(1)}, u32[]{:S(2)}, u32[]{:S(2)}) collective-permute-start(f32[6,20,2,128]{3,2,1,0:T(2,128)S(1)} %get-tuple-element.49), channel_id=1, source_target_pairs={{1,0},{2,1},{3,2},{5,4},{6,5},{7,6},{9,8},{10,9},{11,10},{13,12},{... | collective-permute-start | bytes 368648 | tf_op jit(solution)/shard_map/ppermute | solution.py:20
  117.8 16.9 %copy-start.2 = (f32[3,16,16,128]{3,2,1,0:T(8,128)}, f32[3,16,16,128]{3,2,1,0:T(8,128)S(1)}, u32[]{:S(2)}) copy-start(f32[3,16,16,128]{3,2,1,0:T(8,128)S(1)} %fusion.9) | copy-start | bytes 1179652
  117.9 5.0 %collective-permute-start.20 = (f32[3,2,16,128]{3,2,1,0:T(8,128)S(1)}, f32[3,2,16,128]{3,2,1,0:T(8,128)S(1)}, u32[]{:S(2)}, u32[]{:S(2)}) collective-permute-start(f32[3,2,16,128]{3,2,1,0:T(8,128)S(1)} %get-tuple-element.84), channel_id=1, source_target_pairs={{0,4},{4,8},{8,12},{12,16},{16,20},{20,24},{24,28},{1,5},{5,9},{9,... | collective-permute-start | bytes 147464 | tf_op jit(solution)/shard_map/ppermute | solution.py:18
  121.6 4.1 %collective-permute-start.21 = (f32[3,2,16,128]{3,2,1,0:T(8,128)S(1)}, f32[3,2,16,128]{3,2,1,0:T(8,128)S(1)}, u32[]{:S(2)}, u32[]{:S(2)}) collective-permute-start(f32[3,2,16,128]{3,2,1,0:T(8,128)S(1)} %get-tuple-element.85), channel_id=1, source_target_pairs={{4,0},{8,4},{12,8},{16,12},{20,16},{24,20},{28,24},{5,1},{9,5},{13... | collective-permute-start | bytes 147464 | tf_op jit(solution)/shard_map/ppermute | solution.py:20
  125.7 4.6 %collective-permute-start.22 = (f32[3,20,2,128]{3,2,1,0:T(2,128)S(1)}, f32[3,20,2,128]{3,2,1,0:T(2,128)S(1)}, u32[]{:S(2)}, u32[]{:S(2)}) collective-permute-start(f32[3,20,2,128]{3,2,1,0:T(2,128)S(1)} %get-tuple-element.78), channel_id=1, source_target_pairs={{0,1},{1,2},{2,3},{4,5},{5,6},{6,7},{8,9},{9,10},{10,11},{12,13},{... | collective-permute-start | bytes 184328 | tf_op jit(solution)/shard_map/ppermute | solution.py:18
  128.4 6.1 %collective-permute-start.23 = (f32[3,20,2,128]{3,2,1,0:T(2,128)S(1)}, f32[3,20,2,128]{3,2,1,0:T(2,128)S(1)}, u32[]{:S(2)}, u32[]{:S(2)}) collective-permute-start(f32[3,20,2,128]{3,2,1,0:T(2,128)S(1)} %get-tuple-element.79), channel_id=1, source_target_pairs={{1,0},{2,1},{3,2},{5,4},{6,5},{7,6},{9,8},{10,9},{11,10},{13,12},{... | collective-permute-start | bytes 184328 | tf_op jit(solution)/shard_map/ppermute | solution.py:20
where the time goes:
time: 140 us; the launch traced here: 137 us
  starting transfers between devices  61.4 us (44%)
  waiting for transfers between devices  48.3 us (34%)
  local copies, waits for them, and re-layouts  14.8 us (11%)
  other arithmetic  10 us (7%)
  between operations  1.52 us (1%)
    ppermute x12, waiting for transfers between devices, extended(): lax.ppermute(head, axis, [((i + 1) % count, i) for i in range(ends)])  42.1 us
    ppermute x12, starting transfers between devices, extended(): lax.ppermute(tail, axis, [(i, (i + 1) % count) for i in range(ends)])  37.9 us
    ppermute x12, starting transfers between devices, extended(): lax.ppermute(head, axis, [((i + 1) % count, i) for i in range(ends)])  15.7 us
    slice x34, local copies, waits for them, and re-layouts, window(): return lax.slice_in_dim(values, start_at, start_at + extent, axis=dimension)  5.43 us
    ppermute x12, waiting for transfers between devices, extended(): lax.ppermute(tail, axis, [(i, (i + 1) % count) for i in range(ends)])  5.36 us
    all_to_all x1, starting transfers between devices, local(): lax.all_to_all(cell_buffer, 'gy', split_axis=0, concat_axis=0, tiled=True)  4.53 us
    all_to_all x1, starting transfers between devices, local(): lax.all_to_all(term_buffer.reshape(groups, capacity, -1), 'gy', split_axi...  3.35 us
    unnamed x19, local copies, waits for them, and re-layouts  3 us
  transfers between devices with their start and end apart: 26, of which 18 were waited for; matrix products, arithmetic and copies ran while one was open for 8% of the time, Pallas kernels for 0%

commit v1 on v0

v1 whole, which is shorter than its diff:
```python
import functools

import jax
import jax.numpy as jnp
from jax import lax
from jax.experimental import pallas as pl
from jax.experimental.pallas import tpu as pltpu
from jax.sharding import PartitionSpec as P

A = 9.0 / 8.0
B = -1.0 / 24.0
MESH = pl.DeviceIdType.MESH
XP = 2
YP = 8

STRESS_FACES = (((0, True), (3, False), (4, False)), ((3, False), (1, True), (5, False)))
VELOCITY_FACES = (((0, False), (1, True), (2, True)), ((0, True), (1, False), (2, True)))


def face_layers(faces, up, extent):
    out = []
    for comp, forward in faces:
        if up:
            out += [(comp, extent - 1)] + ([] if forward else [(comp, extent - 2)])
        else:
            out += [(comp, 0)] + ([(comp, 1)] if forward else [])
    return out


def halo_terms(faces, from_low, extent, halo):
    out, at = [], 0
    for comp, forward in faces:
        first = halo(at)
        if from_low:
            if forward:
                out.append((comp, 0, -B * first))
                at += 1
            else:
                second = halo(at + 1)
                out.append((comp, 0, -A * first - B * second))
                out.append((comp, 1, -B * first))
                at += 2
        else:
            if forward:
                second = halo(at + 1)
                out.append((comp, extent - 1, A * first + B * second))
                out.append((comp, extent - 2, B * first))
                at += 2
            else:
                out.append((comp, extent - 1, B * first))
                at += 1
    return out


def kernel(
    groups, blocks, steps,
    v_hbm, s_hbm, buoy_hbm, lame_hbm, rig_hbm, hist_hbm, mech_ref, res_ref, own_ref, off_ref,
    vo_hbm, so_hbm,
    V, S, buoy, lame, rig, hist, src, gathered, plane_hot, level_hot,
    send_x, recv_x, send_y, recv_y,
    load_sem, store_sem, src_send, src_recv, face_send, face_recv,
):
    gx = lax.axis_index("gx")
    gy = lax.axis_index("gy")
    cx, cy, cz = buoy.shape
    rows = hist.shape[0]
    inner = (slice(None), pl.ds(XP, cx), pl.ds(YP, cy), slice(None))

    barrier = pltpu.get_barrier_semaphore()
    sides = (
        (gx > 0, (gx - 1, gy)),
        (gx < blocks - 1, (gx + 1, gy)),
        (gy > 0, (gx, gy - 1)),
        (gy < groups - 1, (gx, gy + 1)),
    )
    for there, device in sides[:2]:
        @pl.when(there)
        def _(device=device):
            pl.semaphore_signal(barrier, inc=1, device_id=device, device_id_type=MESH)
    for k in range(1, groups):
        pl.semaphore_signal(
            barrier, inc=1, device_id=(gx, lax.rem(gy + k, groups)), device_id_type=MESH
        )

    loads = [
        pltpu.make_async_copy(s_hbm, S.at[inner], load_sem.at[0]),
        pltpu.make_async_copy(hist_hbm, hist, load_sem.at[1]),
        pltpu.make_async_copy(v_hbm, V.at[inner], load_sem.at[2]),
        pltpu.make_async_copy(buoy_hbm, buoy, load_sem.at[3]),
        pltpu.make_async_copy(lame_hbm, lame, load_sem.at[4]),
        pltpu.make_async_copy(rig_hbm, rig, load_sem.at[5]),
    ]
    for load in loads:
        load.start()

    for ref in (V, S):
        zero_x = jnp.zeros((ref.shape[0], XP, cy, cz), jnp.float32)
        ref[:, pl.ds(0, XP), pl.ds(YP, cy), :] = zero_x
        ref[:, pl.ds(XP + cx, XP), pl.ds(YP, cy), :] = zero_x

        def clear(x, carry, ref=ref):
            zero_y = jnp.zeros((ref.shape[0], YP, cz), jnp.float32)
            ref[:, XP + x, pl.ds(0, YP), :] = zero_y
            ref[:, XP + x, pl.ds(YP + cy, YP), :] = zero_y
            return carry

        lax.fori_loop(0, cx, clear, 0)

    def face_copy(phase, side, faces):
        axis, up = side // 2, side % 2
        send, recv = ((send_x, recv_x), (send_y, recv_y))[axis]
        count = len(face_layers(faces[axis], bool(up), (cx, cy)[axis]))
        return pltpu.make_async_remote_copy(
            src_ref=send.at[phase, up, pl.ds(0, count)],
            dst_ref=recv.at[phase, up, pl.ds(0, count)],
            send_sem=face_send.at[phase, side],
            recv_sem=face_recv.at[phase, side],
            device_id=sides[side][1],
            device_id_type=MESH,
        )

    def row(ref, comp, axis, layer):
        if axis == 0:
            return ref.at[comp, XP + layer, pl.ds(YP, cy), :]
        return ref.at[comp, pl.ds(XP, cx), YP + layer, :]

    def coefficient(ref, axis, layer):
        return ref[layer] if axis == 0 else ref[:, layer, :]

    def send_faces(phase, ref, faces):
        for side in (3, 2, 1, 0):
            axis, up = side // 2, side % 2
            send = (send_x, send_y)[axis]

            @pl.when(sides[side][0])
            def _():
                for at, (comp, layer) in enumerate(
                    face_layers(faces[axis], bool(up), (cx, cy)[axis])
                ):
                    send[phase, up, at] = row(ref, comp, axis, layer)[...]
                face_copy(phase, side, faces).start()

    def receive_faces(phase, faces, apply):
        for side in (0, 1, 2, 3):
            axis, up = side // 2, side % 2
            recv = (recv_x, recv_y)[axis]

            @pl.when(sides[side][0])
            def _():
                face_copy(phase, 2 * axis + 1 - up, faces).wait_recv()
                for comp, layer, value in halo_terms(
                    faces[axis], not up, (cx, cy)[axis], lambda at: recv[phase, 1 - up, at]
                ):
                    apply(axis, comp, layer, value)

    def finish_faces(phase, faces):
        for side in (0, 1, 2, 3):
            @pl.when(sides[side][0])
            def _():
                face_copy(phase, side, faces).wait_send()

    def add(ref, comp, axis, layer, value):
        place = row(ref, comp, axis, layer)
        place[...] = place[...] + value

    force_of = ({0: 0, 3: 1, 4: 2}, {3: 0, 1: 1, 5: 2})

    def apply_force(axis, comp, layer, value):
        add(V, force_of[axis][comp], axis, layer, coefficient(buoy, axis, layer) * value)

    shear_of = ({1: 3, 2: 4}, {0: 3, 2: 5})

    def apply_strain(axis, comp, layer, value):
        mu = coefficient(rig, axis, layer)
        if comp != axis:
            add(S, shear_of[axis][comp], axis, layer, mu * value)
            return
        volume = coefficient(lame, axis, layer) * value
        for normal in range(3):
            extra = volume + 2.0 * mu * value if normal == axis else volume
            add(S, normal, axis, layer, extra)

    level = lax.broadcasted_iota(jnp.int32, (cy, cz), 1)

    def along_z(values, by):
        moved = pltpu.roll(values, (-by) % cz, 1)
        return jnp.where(level < cz - by if by > 0 else level >= -by, moved, 0.0)

    def differ(ref, comp, x, dimension, forward):
        def window(by):
            if dimension == 0:
                return ref[comp, XP + x + by, pl.ds(YP, cy), :]
            if dimension == 1:
                return ref[comp, XP + x, pl.ds(YP + by, cy), :]
            values = ref[comp, XP + x, pl.ds(YP, cy), :]
            return along_z(values, by) if by else values

        if forward:
            return A * (window(1) - window(0)) + B * (window(2) - window(-1))
        return A * (window(0) - window(-1)) + B * (window(1) - window(-2))

    def velocity_inner(x, carry):
        force = (
            differ(S, 0, x, 0, True) + differ(S, 3, x, 1, False) + differ(S, 4, x, 2, False),
            differ(S, 3, x, 0, False) + differ(S, 1, x, 1, True) + differ(S, 5, x, 2, False),
            differ(S, 4, x, 0, False) + differ(S, 5, x, 1, False) + differ(S, 2, x, 2, True),
        )
        factor = buoy[x]
        for comp in range(3):
            place = V.at[comp, XP + x, pl.ds(YP, cy), :]
            place[...] = place[...] + factor * force[comp]
        return carry

    def stress_inner(x, carry):
        one = differ(V, 0, x, 0, False)
        two = differ(V, 1, x, 1, False)
        three = differ(V, 2, x, 2, False)
        mu = rig[x]
        volume = lame[x] * (one + two + three)
        rates = (
            volume + 2.0 * mu * one,
            volume + 2.0 * mu * two,
            volume + 2.0 * mu * three,
            mu * (differ(V, 0, x, 1, True) + differ(V, 1, x, 0, True)),
            mu * (differ(V, 0, x, 2, True) + differ(V, 2, x, 0, True)),
            mu * (differ(V, 1, x, 2, True) + differ(V, 2, x, 1, True)),
        )
        for comp in range(6):
            place = S.at[comp, XP + x, pl.ds(YP, cy), :]
            place[...] = place[...] + rates[comp]
        return carry

    def source_copy(k):
        return pltpu.make_async_remote_copy(
            src_ref=src,
            dst_ref=gathered.at[:, pl.ds(k * rows, rows)],
            send_sem=src_send.at[k],
            recv_sem=src_recv.at[k],
            device_id=(gx, lax.rem(gy + k, groups)),
            device_id_type=MESH,
        )

    def source_terms():
        contract_last = (((1,), (1,)), ((), ()))
        amplitude = lax.dot_general(
            res_ref[...], hist[...], contract_last, preferred_element_type=jnp.float32
        )
        comps = mech_ref.shape[0]
        parts = [mech_ref[...].astype(jnp.float32) * amplitude[t : t + 1, :] for t in range(steps)]
        offsets = off_ref[...]
        places = [own_ref[...], offsets // (cy * cz), (offsets // cz) % cy, offsets % cz]
        places = [p.astype(jnp.float32) for p in places]
        parts += [jnp.concatenate(places + [jnp.zeros((comps - 4, rows), jnp.float32)], axis=0)]
        packed = jnp.concatenate(parts, axis=0).astype(jnp.bfloat16)
        src[...] = packed
        gathered[:, pl.ds(0, rows)] = packed

    comps = mech_ref.shape[0]

    def source_masks():
        for k in range(groups):
            lanes = pl.ds(k * rows, rows)
            info = gathered[pl.ds(steps * comps, comps), lanes].astype(jnp.float32)
            cell_plane = info[0:1] * float(cx * cy) + info[1:2] * float(cy) + info[2:3]
            plane = lax.broadcasted_iota(jnp.int32, (cx * cy, rows), 0) + gy * (cx * cy)
            plane_hot[:, lanes] = jnp.where(
                plane == cell_plane.astype(jnp.int32), 1.0, 0.0
            ).astype(jnp.bfloat16)
            height = lax.broadcasted_iota(jnp.int32, (cz, rows), 0)
            level_hot[:, lanes] = jnp.where(
                height == info[3:4].astype(jnp.int32), 1.0, 0.0
            ).astype(jnp.bfloat16)

    def insert_sources(t):
        values = gathered[pl.ds(t * comps, comps), :].astype(jnp.float32)
        for comp in range(0, 6, 2):
            spread = jnp.concatenate(
                [
                    level_hot[...] * values[c : c + 1, :].astype(jnp.bfloat16)
                    for c in (comp, comp + 1)
                ],
                axis=0,
            )
            placed = lax.dot_general(
                plane_hot[...], spread, (((1,), (1,)), ((), ())),
                preferred_element_type=jnp.float32,
            )
            for c in range(2):
                place = S.at[comp + c, pl.ds(XP, cx), pl.ds(YP, cy), :]
                place[...] = place[...] + placed[:, c * cz : (c + 1) * cz].reshape(cx, cy, cz)

    arrivals = (
        (gx > 0).astype(jnp.int32) + (gx < blocks - 1).astype(jnp.int32) + (groups - 1)
    )
    loads[0].wait()
    pl.semaphore_wait(barrier, arrivals)
    for t in range(steps):
        first, second = 2 * t, 2 * t + 1
        send_faces(first, S, STRESS_FACES)
        if t == 0:
            loads[1].wait()
            source_terms()
            for k in range(1, groups):
                source_copy(k).start()
            loads[2].wait()
            loads[3].wait()
        lax.fori_loop(0, cx, velocity_inner, 0)
        if t > 0:
            insert_sources(t)
        receive_faces(first, STRESS_FACES, apply_force)
        send_faces(second, V, VELOCITY_FACES)
        if t == steps - 1:
            store_v = pltpu.make_async_copy(V.at[inner], vo_hbm, store_sem.at[0])
            store_v.start()
        if t == 0:
            loads[4].wait()
            loads[5].wait()
        lax.fori_loop(0, cx, stress_inner, 0)
        if t == 0:
            for k in range(1, groups):
                source_copy(k).wait_recv()
            source_masks()
            insert_sources(0)
        receive_faces(second, VELOCITY_FACES, apply_strain)
    store_s = pltpu.make_async_copy(S.at[inner], so_hbm, store_sem.at[1])
    store_s.start()
    for t in range(steps):
        finish_faces(2 * t, STRESS_FACES)
        finish_faces(2 * t + 1, VELOCITY_FACES)
    for k in range(1, groups):
        source_copy(k).wait_send()
    store_v.wait()
    store_s.wait()


def local(
    velocity, stresses, buoyancy, lame_first, rigidity,
    histories, mechanism, resample, owners, cell_offsets,
):
    groups = lax.axis_size("gy")
    blocks = lax.axis_size("gx")
    rows, samples = histories.shape
    steps = resample.shape[1]
    _, cx, cy, cz = velocity.shape
    comps = 8
    tall = comps * (steps + 1)
    f32, bf16 = jnp.float32, jnp.bfloat16
    mech = jnp.pad(mechanism.T, ((0, comps - mechanism.shape[1]), (0, 0)))
    res = jnp.pad(resample.T, ((0, -steps % 8), (0, 0)))
    hbm = pl.BlockSpec(memory_space=pl.ANY)
    vmem = pl.BlockSpec(memory_space=pltpu.VMEM)
    dma = pltpu.SemaphoreType.DMA
    phases = 2 * steps
    return pl.pallas_call(
        functools.partial(kernel, groups, blocks, steps),
        out_shape=(
            jax.ShapeDtypeStruct(velocity.shape, f32),
            jax.ShapeDtypeStruct(stresses.shape, f32),
        ),
        in_specs=[hbm] * 6 + [vmem] * 4,
        out_specs=(hbm, hbm),
        scratch_shapes=[
            pltpu.VMEM((3, cx + 2 * XP, cy + 2 * YP, cz), f32),
            pltpu.VMEM((6, cx + 2 * XP, cy + 2 * YP, cz), f32),
            pltpu.VMEM((cx, cy, cz), f32),
            pltpu.VMEM((cx, cy, cz), f32),
            pltpu.VMEM((cx, cy, cz), f32),
            pltpu.VMEM((rows, samples), bf16),
            pltpu.VMEM((tall, rows), bf16),
            pltpu.VMEM((tall, groups * rows), bf16),
            pltpu.VMEM((cx * cy, groups * rows), bf16),
            pltpu.VMEM((cz, groups * rows), bf16),
            pltpu.VMEM((phases, 2, 5, cy, cz), f32),
            pltpu.VMEM((phases, 2, 5, cy, cz), f32),
            pltpu.VMEM((phases, 2, 5, cx, cz), f32),
            pltpu.VMEM((phases, 2, 5, cx, cz), f32),
            dma((6,)),
            dma((2,)),
            dma((groups,)),
            dma((groups,)),
            dma((phases, 4)),
            dma((phases, 4)),
        ],
        compiler_params=pltpu.CompilerParams(collective_id=0, has_side_effects=True),
    )(
        velocity, stresses, buoyancy, lame_first, rigidity, histories, mech, res,
        owners.reshape(1, rows), cell_offsets.reshape(1, rows),
    )


def solution(mesh):
    in_specs = (
        P(None, "gx", "gy", None),
        P(None, "gx", "gy", None),
        P("gx", "gy", None),
        P("gx", "gy", None),
        P("gx", "gy", None),
        P(("gx", "gy"), None),
        P(("gx", "gy"), None),
        P(),
        P(("gx", "gy"), None),
        P(("gx", "gy")),
    )
    out_specs = (P(None, "gx", "gy", None), P(None, "gx", "gy", None))
    return jax.shard_map(local, mesh=mesh, in_specs=in_specs, out_specs=out_specs, check_vma=False)
```

time: 140 us -> 34.5 us (0.25); the launches traced: 137 us -> 34.2 us
  starting transfers between devices: 61.4 us -> 0 us
  waiting for transfers between devices: 48.3 us -> 0 us
  Pallas kernels: 0 us -> 28.9 us
  local copies, waits for them, and re-layouts: 14.8 us -> 4.7 us
  other arithmetic: 10 us -> 0 us
    ppermute x24 -> x0, starting transfers between devices: 53.6 us -> none  [the longest x12 37.9 us: extended(): lax.ppermute(tail, axis, [(i, (i + 1) % count) for i in range(ends)])]
    ppermute x24 -> x0, waiting for transfers between devices: 47.4 us -> none  [the longest x12 42.1 us: extended(): lax.ppermute(head, axis, [((i + 1) % count, i) for i in range(ends)])]
    pallas_call x0 -> x1, Pallas kernels: none -> 28.9 us  [local(): pl.pallas_call(functools.partial(kernel, groups, blocks, steps), out_shap...]
    all_to_all x2 -> x0, starting transfers between devices: 7.88 us -> none  [the longest x1 4.53 us: local(): lax.all_to_all(cell_buffer, 'gy', split_axis=0, concat_axis=0, tiled=True)]
    slice x44 -> x0, local copies, waits for them, and re-layouts: 6.9 us -> none  [the longest x34 5.43 us: window(): return lax.slice_in_dim(values, start_at, start_at + extent, axis=dimension)]
    scatter x2 -> x0, local copies, waits for them, and re-layouts: 2.73 us -> none  [the longest x1 1.55 us: local(): cell_buffer = jnp.zeros((groups * capacity,), jnp.int32).at[slots].set(ce...]
    another operation x14 -> x0, other arithmetic: 2.71 us -> none
    convert_element_type x4 -> x0, other arithmetic: 1.43 us -> none  [the longest x1 0.69 us: local(): mechanism.astype(jnp.float32)[:, :, None] * amplitude[:, None, :]]
  transfers between devices with their start and end apart: 26 -> 0, of which waited for: 18 -> 0; matrix products, arithmetic and copies ran while one was open for 8% -> 0% of each run, Pallas kernels for 0% -> 0%
where the time goes in v1:
time: 34.5 us; the launch traced here: 34.2 us
  Pallas kernels  28.9 us (84%)
  local copies, waits for them, and re-layouts  4.7 us (14%)
  between operations  0.66 us (2%)
    pallas_call x1, Pallas kernels, local(): pl.pallas_call(functools.partial(kernel, groups, blocks, steps), out_shap...  28.9 us
    unnamed x8, local copies, waits for them, and re-layouts  3.5 us

profile of v1, /device:TPU:0, one launch (start us, length us, event | category | flops | bytes accessed | tf_op | source)
XLA Modules:
  0.0 34.2 jit_solution(12434609207586535792)
XLA Ops:
  0.6 0.0 copy-start.2
  0.6 0.7 %copy-done.2 = bf16[256,6]{0,1:T(8,128)(2,1)S(1)} copy-done((bf16[256,6]{0,1:T(8,128)(2,1)S(1)}, bf16[256,6]{0,1:T(8,128)(2,1)}, u32[]{:S(2)}) %copy-start.2) | copy-done | bytes 3096
  1.3 0.0 copy-start.1
  1.3 0.6 %pad.8.mech_ref = bf16[8,256]{1,0:T(8,128)(2,1)} pad(bf16[6,256]{1,0:T(8,128)(2,1)S(1)} %bitcast.5, bf16[]{:T(256)} %constant.2.clone.1), padding=0_2x0_0 | pad | bytes 7170 | tf_op jit(solution)/shard_map/jit(_pad)/pad | solution.py:348
  1.9 0.1 copy-done.1
  2.0 0.6 %pad.9.res_ref = bf16[8,512]{1,0:T(8,128)(2,1)} pad(bf16[3,512]{1,0:T(4,128)(2,1)S(1)} %bitcast.4, bf16[]{:T(256)} %constant.2.clone.1), padding=0_5x0_0 | pad | bytes 11266 | tf_op jit(solution)/shard_map/jit(_pad)/pad | solution.py:349
  2.6 28.9 %shard_map.113 = (f32[3,16,16,128]{3,2,1,0:T(8,128)}, f32[6,16,16,128]{3,2,1,0:T(8,128)}) custom-call(f32[3,16,16,128]{3,2,1,0:T(8,128)} %v_hbm.1, f32[6,16,16,128]{3,2,1,0:T(8,128)} %s_hbm.1, f32[16,16,128]{2,1,0:T(8,128)} %buoy_hbm.1, f32[16,16,128]{2,1,0:T(8,128)} %lame_hbm.1, f32[16,16,128]{2,1,0:T(8,128)} %rig_hbm.1, bf16[256,512]{1,0:T(8,128)(2,1)} %hist_hbm.1, ...), custom_call_target="tpu_custom_call" | custom-call | tf_op jit(solution)/shard_map/pallas_call | solution.py:354
  31.5 0.0 copy-start
  31.5 1.8 %copy.14 = f32[3,16,16,128]{3,2,1,0:T(8,128)} copy(f32[3,16,16,128]{3,2,1,0:T(8,128)} %get-tuple-element.4) | data formatting | bytes 786432
  33.4 0.0 copy-done
  33.4 0.9 %copy.15 = f32[6,16,16,128]{3,2,1,0:T(8,128)} copy(f32[6,16,16,128]{3,2,1,0:T(8,128)S(1)} %copy-done) | data formatting | bytes 1572864
Async XLA Ops:
  0.6 0.7 %copy-start.2 = (bf16[256,6]{0,1:T(8,128)(2,1)S(1)}, bf16[256,6]{0,1:T(8,128)(2,1)}, u32[]{:S(2)}) copy-start(bf16[256,6]{0,1:T(8,128)(2,1)} %param.16) | copy-start | bytes 9220
  1.3 0.7 %copy-start.1 = (bf16[512,3]{0,1:T(4,128)(2,1)S(1)}, bf16[512,3]{0,1:T(4,128)(2,1)}, u32[]{:S(2)}) copy-start(bf16[512,3]{0,1:T(4,128)(2,1)} %param.17) | copy-start | bytes 9220
  31.5 1.9 %copy-start = (f32[6,16,16,128]{3,2,1,0:T(8,128)S(1)}, f32[6,16,16,128]{3,2,1,0:T(8,128)}, u32[]{:S(2)}) copy-start(f32[6,16,16,128]{3,2,1,0:T(8,128)} %get-tuple-element.5) | copy-start | bytes 2359300

commit v2 on v1

--- a/solution.py
+++ b/solution.py
@@ -54,11 +54,11 @@
 
 def kernel(
     groups, blocks, steps,
-    v_hbm, s_hbm, buoy_hbm, lame_hbm, rig_hbm, hist_hbm, mech_ref, res_ref, own_ref, off_ref,
-    vo_hbm, so_hbm,
-    V, S, buoy, lame, rig, hist, src, gathered, plane_hot, level_hot,
+    v_hbm, s_hbm, buoy_hbm, lame_hbm, rig_hbm, hist_hbm, mech_hbm, res_hbm, own_hbm, off_hbm,
+    v_out, s_out,
+    V, S, buoy, lame, rig, hist, mech_ref, res_ref, own_ref, off_ref, src, gathered, plane_hot, level_hot,
     send_x, recv_x, send_y, recv_y,
-    load_sem, store_sem, src_send, src_recv, face_send, face_recv,
+    load_sem, src_send, src_recv, face_send, face_recv,
 ):
     gx = lax.axis_index("gx")
     gy = lax.axis_index("gy")
@@ -89,6 +89,10 @@
         pltpu.make_async_copy(buoy_hbm, buoy, load_sem.at[3]),
         pltpu.make_async_copy(lame_hbm, lame, load_sem.at[4]),
         pltpu.make_async_copy(rig_hbm, rig, load_sem.at[5]),
+        pltpu.make_async_copy(mech_hbm, mech_ref, load_sem.at[6]),
+        pltpu.make_async_copy(res_hbm, res_ref, load_sem.at[7]),
+        pltpu.make_async_copy(own_hbm, own_ref, load_sem.at[8]),
+        pltpu.make_async_copy(off_hbm, off_ref, load_sem.at[9]),
     ]
     for load in loads:
         load.start()
@@ -120,43 +124,56 @@
         )
 
     def row(ref, comp, axis, layer):
+        x, y = (XP, YP) if ref is V or ref is S else (0, 0)
         if axis == 0:
-            return ref.at[comp, XP + layer, pl.ds(YP, cy), :]
-        return ref.at[comp, pl.ds(XP, cx), YP + layer, :]
+            return ref.at[comp, x + layer, pl.ds(y, cy), :]
+        return ref.at[comp, pl.ds(x, cx), y + layer, :]
 
     def coefficient(ref, axis, layer):
         return ref[layer] if axis == 0 else ref[:, layer, :]
 
-    def send_faces(phase, ref, faces):
-        for side in (3, 2, 1, 0):
-            axis, up = side // 2, side % 2
-            send = (send_x, send_y)[axis]
-
-            @pl.when(sides[side][0])
-            def _():
-                for at, (comp, layer) in enumerate(
-                    face_layers(faces[axis], bool(up), (cx, cy)[axis])
-                ):
-                    send[phase, up, at] = row(ref, comp, axis, layer)[...]
-                face_copy(phase, side, faces).start()
-
-    def receive_faces(phase, faces, apply):
-        for side in (0, 1, 2, 3):
-            axis, up = side // 2, side % 2
-            recv = (recv_x, recv_y)[axis]
-
-            @pl.when(sides[side][0])
-            def _():
-                face_copy(phase, 2 * axis + 1 - up, faces).wait_recv()
-                for comp, layer, value in halo_terms(
-                    faces[axis], not up, (cx, cy)[axis], lambda at: recv[phase, 1 - up, at]
-                ):
-                    apply(axis, comp, layer, value)
+    odd = lax.rem(gy, 2) == 1
+    even = jnp.logical_not(odd)
+    near = ((2, jnp.logical_and(sides[2][0], odd)), (3, jnp.logical_and(sides[3][0], even)))
+    far = ((3, jnp.logical_and(sides[3][0], odd)), (2, jnp.logical_and(sides[2][0], even)))
+    across = ((0, sides[0][0]), (1, sides[1][0]))
+
+    def send_face(side, phase, ref, faces):
+        axis, up = side // 2, side % 2
+        send = (send_x, send_y)[axis]
+        for at, (comp, layer) in enumerate(face_layers(faces[axis], bool(up), (cx, cy)[axis])):
+            send[phase, up, at] = row(ref, comp, axis, layer)[...]
+        face_copy(phase, side, faces).start()
+
+    def receive_face(side, phase, faces, apply):
+        axis, up = side // 2, side % 2
+        recv = (recv_x, recv_y)[axis]
+        face_copy(phase, 2 * axis + 1 - up, faces).wait_recv()
+        for comp, layer, value in halo_terms(
+            faces[axis], not up, (cx, cy)[axis], lambda at: recv[phase, 1 - up, at]
+        ):
+            apply(axis, comp, layer, value)
+
+    def at_sides(which, *actions):
+        for side, there in which:
+            @pl.when(there)
+            def _(side=side):
+                for action in actions:
+                    action(side)
+
+    def exchange(phase, faces, apply, send):
+        def receive(side):
+            receive_face(side, phase, faces, apply)
+
+        at_sides(across, receive)
+        at_sides(near, receive, *send)
+        at_sides(far, receive, *send)
+        at_sides(across, *send)
 
     def finish_faces(phase, faces):
         for side in (0, 1, 2, 3):
             @pl.when(sides[side][0])
-            def _():
+            def _(side=side):
                 face_copy(phase, side, faces).wait_send()
 
     def add(ref, comp, axis, layer, value):
@@ -170,15 +187,15 @@
 
     shear_of = ({1: 3, 2: 4}, {0: 3, 2: 5})
 
-    def apply_strain(axis, comp, layer, value):
+    def apply_strain(target, axis, comp, layer, value):
         mu = coefficient(rig, axis, layer)
         if comp != axis:
-            add(S, shear_of[axis][comp], axis, layer, mu * value)
+            add(target, shear_of[axis][comp], axis, layer, mu * value)
             return
         volume = coefficient(lame, axis, layer) * value
         for normal in range(3):
             extra = volume + 2.0 * mu * value if normal == axis else volume
-            add(S, normal, axis, layer, extra)
+            add(target, normal, axis, layer, extra)
 
     level = lax.broadcasted_iota(jnp.int32, (cy, cz), 1)
 
@@ -211,7 +228,7 @@
             place[...] = place[...] + factor * force[comp]
         return carry
 
-    def stress_inner(x, carry):
+    def stress_inner(last, x, carry):
         one = differ(V, 0, x, 0, False)
         two = differ(V, 1, x, 1, False)
         three = differ(V, 2, x, 2, False)
@@ -227,7 +244,11 @@
         )
         for comp in range(6):
             place = S.at[comp, XP + x, pl.ds(YP, cy), :]
-            place[...] = place[...] + rates[comp]
+            target = s_out.at[comp, x] if last else place
+            target[...] = place[...] + rates[comp]
+        if last:
+            for comp in range(3):
+                v_out[comp, x] = V[comp, XP + x, pl.ds(YP, cy), :]
         return carry
 
     def source_copy(k):
@@ -240,13 +261,18 @@
             device_id_type=MESH,
         )
 
+    comps = src.shape[0] // (steps + 1)
+
     def source_terms():
         contract_last = (((1,), (1,)), ((), ()))
         amplitude = lax.dot_general(
             res_ref[...], hist[...], contract_last, preferred_element_type=jnp.float32
         )
-        comps = mech_ref.shape[0]
-        parts = [mech_ref[...].astype(jnp.float32) * amplitude[t : t + 1, :] for t in range(steps)]
+        mech = mech_ref[...].astype(jnp.float32)
+        spare = jnp.zeros((comps - mech.shape[0], rows), jnp.float32)
+        parts = []
+        for t in range(steps):
+            parts += [mech * amplitude[t : t + 1, :], spare]
         offsets = off_ref[...]
         places = [own_ref[...], offsets // (cy * cz), (offsets // cz) % cy, offsets % cz]
         places = [p.astype(jnp.float32) for p in places]
@@ -254,8 +280,6 @@
         packed = jnp.concatenate(parts, axis=0).astype(jnp.bfloat16)
         src[...] = packed
         gathered[:, pl.ds(0, rows)] = packed
-
-    comps = mech_ref.shape[0]
 
     def source_masks():
         for k in range(groups):
@@ -294,43 +318,53 @@
     )
     loads[0].wait()
     pl.semaphore_wait(barrier, arrivals)
+
+    def send_stress(phase):
+        return lambda side: send_face(side, phase, S, STRESS_FACES)
+
+    def send_velocity(phase):
+        return lambda side: send_face(side, phase, V, VELOCITY_FACES)
+
+    for which in (far, near, across):
+        at_sides(which, send_stress(0))
+    for load in (loads[1],) + tuple(loads[6:]):
+        load.wait()
+    source_terms()
+    for k in range(1, groups):
+        source_copy(k).start()
+    loads[2].wait()
+    loads[3].wait()
     for t in range(steps):
         first, second = 2 * t, 2 * t + 1
-        send_faces(first, S, STRESS_FACES)
-        if t == 0:
-            loads[1].wait()
-            source_terms()
-            for k in range(1, groups):
-                source_copy(k).start()
-            loads[2].wait()
-            loads[3].wait()
+        last = t == steps - 1
         lax.fori_loop(0, cx, velocity_inner, 0)
         if t > 0:
             insert_sources(t)
-        receive_faces(first, STRESS_FACES, apply_force)
-        send_faces(second, V, VELOCITY_FACES)
-        if t == steps - 1:
-            store_v = pltpu.make_async_copy(V.at[inner], vo_hbm, store_sem.at[0])
-            store_v.start()
+        exchange(first, STRESS_FACES, apply_force, (send_velocity(second),))
         if t == 0:
             loads[4].wait()
             loads[5].wait()
-        lax.fori_loop(0, cx, stress_inner, 0)
-        if t == 0:
+        if t == 0 and last:
             for k in range(1, groups):
                 source_copy(k).wait_recv()
             source_masks()
             insert_sources(0)
-        receive_faces(second, VELOCITY_FACES, apply_strain)
-    store_s = pltpu.make_async_copy(S.at[inner], so_hbm, store_sem.at[1])
-    store_s.start()
+        lax.fori_loop(0, cx, functools.partial(stress_inner, last), 0)
+        if t == 0 and not last:
+            for k in range(1, groups):
+                source_copy(k).wait_recv()
+            source_masks()
+            insert_sources(0)
+        exchange(
+            second, VELOCITY_FACES,
+            functools.partial(apply_strain, s_out if last else S),
+            () if last else (send_stress(second + 1),),
+        )
     for t in range(steps):
         finish_faces(2 * t, STRESS_FACES)
         finish_faces(2 * t + 1, VELOCITY_FACES)
     for k in range(1, groups):
         source_copy(k).wait_send()
-    store_v.wait()
-    store_s.wait()
 
 
 def local(
@@ -345,8 +379,6 @@
     comps = 8
     tall = comps * (steps + 1)
     f32, bf16 = jnp.float32, jnp.bfloat16
-    mech = jnp.pad(mechanism.T, ((0, comps - mechanism.shape[1]), (0, 0)))
-    res = jnp.pad(resample.T, ((0, -steps % 8), (0, 0)))
     hbm = pl.BlockSpec(memory_space=pl.ANY)
     vmem = pl.BlockSpec(memory_space=pltpu.VMEM)
     dma = pltpu.SemaphoreType.DMA
@@ -354,11 +386,11 @@
     return pl.pallas_call(
         functools.partial(kernel, groups, blocks, steps),
         out_shape=(
-            jax.ShapeDtypeStruct(velocity.shape, f32),
-            jax.ShapeDtypeStruct(stresses.shape, f32),
+            pltpu.VMEM(velocity.shape, f32),
+            pltpu.VMEM(stresses.shape, f32),
         ),
-        in_specs=[hbm] * 6 + [vmem] * 4,
-        out_specs=(hbm, hbm),
+        in_specs=[hbm] * 10,
+        out_specs=(vmem, vmem),
         scratch_shapes=[
             pltpu.VMEM((3, cx + 2 * XP, cy + 2 * YP, cz), f32),
             pltpu.VMEM((6, cx + 2 * XP, cy + 2 * YP, cz), f32),
@@ -366,6 +398,10 @@
             pltpu.VMEM((cx, cy, cz), f32),
             pltpu.VMEM((cx, cy, cz), f32),
             pltpu.VMEM((rows, samples), bf16),
+            pltpu.VMEM((mechanism.shape[1], rows), bf16),
+            pltpu.VMEM((steps, samples), bf16),
+            pltpu.VMEM((1, rows), jnp.int32),
+            pltpu.VMEM((1, rows), jnp.int32),
             pltpu.VMEM((tall, rows), bf16),
             pltpu.VMEM((tall, groups * rows), bf16),
             pltpu.VMEM((cx * cy, groups * rows), bf16),
@@ -374,8 +410,7 @@
             pltpu.VMEM((phases, 2, 5, cy, cz), f32),
             pltpu.VMEM((phases, 2, 5, cx, cz), f32),
             pltpu.VMEM((phases, 2, 5, cx, cz), f32),
-            dma((6,)),
-            dma((2,)),
+            dma((10,)),
             dma((groups,)),
             dma((groups,)),
             dma((phases, 4)),
@@ -383,7 +418,7 @@
         ],
         compiler_params=pltpu.CompilerParams(collective_id=0, has_side_effects=True),
     )(
-        velocity, stresses, buoyancy, lame_first, rigidity, histories, mech, res,
+        velocity, stresses, buoyancy, lame_first, rigidity, histories, mechanism.T, resample.T,
         owners.reshape(1, rows), cell_offsets.reshape(1, rows),
     )
 

time: 34.5 us -> 27.5 us (0.80)
  Pallas kernels: 28.9 us -> 24.8 us
  local copies, waits for them, and re-layouts: 4.7 us -> 1.63 us
    pallas_call x1, Pallas kernels: 28.9 us -> 24.8 us  [local(): pl.pallas_call(functools.partial(kernel, groups, blocks, steps), out_shap...]
    unnamed x8 -> x2, local copies, waits for them, and re-layouts: 3.5 us -> 1.63 us
    pad x2 -> x0, local copies, waits for them, and re-layouts: 1.2 us -> none  [the longest x1 0.6 us: local(): res = jnp.pad(resample.T, ((0, -steps % 8), (0, 0)))]
where the time goes in v2:
time: 27.5 us; the launch traced here: 27.1 us
  Pallas kernels  24.8 us (90%)
  local copies, waits for them, and re-layouts  1.63 us (6%)
  between operations  0.64 us (2%)
    pallas_call x1, Pallas kernels, local(): pl.pallas_call(functools.partial(kernel, groups, blocks, steps), out_shap...  24.8 us
    unnamed x2, local copies, waits for them, and re-layouts  1.63 us

profile of v2, /device:TPU:0, one launch (start us, length us, event | category | flops | bytes accessed | tf_op | source)
XLA Modules:
  0.0 27.1 jit_solution(12565589458872402876)
XLA Ops:
  0.6 24.8 %shard_map.113 = (f32[3,16,16,128]{3,2,1,0:T(8,128)S(1)}, f32[6,16,16,128]{3,2,1,0:T(8,128)S(1)}) custom-call(f32[3,16,16,128]{3,2,1,0:T(8,128)} %v_hbm.1, f32[6,16,16,128]{3,2,1,0:T(8,128)} %s_hbm.1, f32[16,16,128]{2,1,0:T(8,128)} %buoy_hbm.1, f32[16,16,128]{2,1,0:T(8,128)} %lame_hbm.1, f32[16,16,128]{2,1,0:T(8,128)} %rig_hbm.1, bf16[256,512]{1,0:T(8,128)(2,1)} %hist_hbm.1, ...), custom_call_target="tpu_custom_call" | custom-call | tf_op jit(solution)/shard_map/pallas_call | solution.py:386
  25.4 0.7 %copy.14 = f32[3,16,16,128]{3,2,1,0:T(8,128)} copy(f32[3,16,16,128]{3,2,1,0:T(8,128)S(1)} %get-tuple-element.2) | data formatting | bytes 786432
  26.2 0.9 %copy.15 = f32[6,16,16,128]{3,2,1,0:T(8,128)} copy(f32[6,16,16,128]{3,2,1,0:T(8,128)S(1)} %get-tuple-element.3) | data formatting | bytes 1572864

commit v3 on v2

--- a/solution.py
+++ b/solution.py
@@ -21,34 +21,34 @@
     out = []
     for comp, forward in faces:
         if up:
-            out += [(comp, extent - 1)] + ([] if forward else [(comp, extent - 2)])
+            out += [(comp, extent - 1, not forward)]
+            out += [] if forward else [(comp, extent - 2, False)]
         else:
-            out += [(comp, 0)] + ([(comp, 1)] if forward else [])
+            out += [(comp, 0, forward)]
+            out += [(comp, 1, False)] if forward else []
     return out
+
+
+def face_slots(faces, up, extent):
+    return sum(2 if wide else 1 for _, _, wide in face_layers(faces, up, extent))
 
 
 def halo_terms(faces, from_low, extent, halo):
     out, at = [], 0
     for comp, forward in faces:
-        first = halo(at)
+        if from_low == forward:
+            sign = -B if from_low else B
+            out.append((comp, 0 if from_low else extent - 1, sign * halo(at)))
+            at += 1
+            continue
+        first, second = halo(at) + halo(at + 1), halo(at + 2)
+        at += 3
         if from_low:
-            if forward:
-                out.append((comp, 0, -B * first))
-                at += 1
-            else:
-                second = halo(at + 1)
-                out.append((comp, 0, -A * first - B * second))
-                out.append((comp, 1, -B * first))
-                at += 2
+            out.append((comp, 0, -A * first - B * second))
+            out.append((comp, 1, -B * first))
         else:
-            if forward:
-                second = halo(at + 1)
-                out.append((comp, extent - 1, A * first + B * second))
-                out.append((comp, extent - 2, B * first))
-                at += 2
-            else:
-                out.append((comp, extent - 1, B * first))
-                at += 1
+            out.append((comp, extent - 1, A * first + B * second))
+            out.append((comp, extent - 2, B * first))
     return out
 
 
@@ -58,7 +58,7 @@
     v_out, s_out,
     V, S, buoy, lame, rig, hist, mech_ref, res_ref, own_ref, off_ref, src, gathered, plane_hot, level_hot,
     send_x, recv_x, send_y, recv_y,
-    load_sem, src_send, src_recv, face_send, face_recv,
+    stress_sem, load_sem, src_send, src_recv, face_send, face_recv,
 ):
     gx = lax.axis_index("gx")
     gy = lax.axis_index("gy")
@@ -83,18 +83,23 @@
         )
 
     loads = [
-        pltpu.make_async_copy(s_hbm, S.at[inner], load_sem.at[0]),
-        pltpu.make_async_copy(hist_hbm, hist, load_sem.at[1]),
-        pltpu.make_async_copy(v_hbm, V.at[inner], load_sem.at[2]),
-        pltpu.make_async_copy(buoy_hbm, buoy, load_sem.at[3]),
-        pltpu.make_async_copy(lame_hbm, lame, load_sem.at[4]),
-        pltpu.make_async_copy(rig_hbm, rig, load_sem.at[5]),
-        pltpu.make_async_copy(mech_hbm, mech_ref, load_sem.at[6]),
-        pltpu.make_async_copy(res_hbm, res_ref, load_sem.at[7]),
-        pltpu.make_async_copy(own_hbm, own_ref, load_sem.at[8]),
-        pltpu.make_async_copy(off_hbm, off_ref, load_sem.at[9]),
+        pltpu.make_async_copy(hist_hbm, hist, load_sem.at[0]),
+        pltpu.make_async_copy(v_hbm, V.at[inner], load_sem.at[1]),
+        pltpu.make_async_copy(buoy_hbm, buoy, load_sem.at[2]),
+        pltpu.make_async_copy(lame_hbm, lame, load_sem.at[3]),
+        pltpu.make_async_copy(rig_hbm, rig, load_sem.at[4]),
+        pltpu.make_async_copy(mech_hbm, mech_ref, load_sem.at[5]),
+        pltpu.make_async_copy(res_hbm, res_ref, load_sem.at[6]),
+        pltpu.make_async_copy(own_hbm, own_ref, load_sem.at[7]),
+        pltpu.make_async_copy(off_hbm, off_ref, load_sem.at[8]),
     ]
-    for load in loads:
+    stress_loads = {
+        comp: pltpu.make_async_copy(
+            s_hbm.at[comp], S.at[(comp,) + inner[1:]], stress_sem.at[comp]
+        )
+        for comp in (3, 1, 5, 0, 4, 2)
+    }
+    for load in list(stress_loads.values()) + loads:
         load.start()
 
     for ref in (V, S):
@@ -113,7 +118,7 @@
     def face_copy(phase, side, faces):
         axis, up = side // 2, side % 2
         send, recv = ((send_x, recv_x), (send_y, recv_y))[axis]
-        count = len(face_layers(faces[axis], bool(up), (cx, cy)[axis]))
+        count = face_slots(faces[axis], bool(up), (cx, cy)[axis])
         return pltpu.make_async_remote_copy(
             src_ref=send.at[phase, up, pl.ds(0, count)],
             dst_ref=recv.at[phase, up, pl.ds(0, count)],
@@ -141,8 +146,15 @@
     def send_face(side, phase, ref, faces):
         axis, up = side // 2, side % 2
         send = (send_x, send_y)[axis]
-        for at, (comp, layer) in enumerate(face_layers(faces[axis], bool(up), (cx, cy)[axis])):
-            send[phase, up, at] = row(ref, comp, axis, layer)[...]
+        at = 0
+        for comp, layer, wide in face_layers(faces[axis], bool(up), (cx, cy)[axis]):
+            value = row(ref, comp, axis, layer)[...]
+            head = value.astype(jnp.bfloat16)
+            send[phase, up, at] = head
+            if wide:
+                rest = value - head.astype(jnp.float32)
+                send[phase, up, at + 1] = rest.astype(jnp.bfloat16)
+            at += 2 if wide else 1
         face_copy(phase, side, faces).start()
 
     def receive_face(side, phase, faces, apply):
@@ -150,7 +162,7 @@
         recv = (recv_x, recv_y)[axis]
         face_copy(phase, 2 * axis + 1 - up, faces).wait_recv()
         for comp, layer, value in halo_terms(
-            faces[axis], not up, (cx, cy)[axis], lambda at: recv[phase, 1 - up, at]
+            faces[axis], not up, (cx, cy)[axis], lambda at: recv[phase, 1 - up, at].astype(jnp.float32)
         ):
             apply(axis, comp, layer, value)
 
@@ -316,7 +328,6 @@
     arrivals = (
         (gx > 0).astype(jnp.int32) + (gx < blocks - 1).astype(jnp.int32) + (groups - 1)
     )
-    loads[0].wait()
     pl.semaphore_wait(barrier, arrivals)
 
     def send_stress(phase):
@@ -325,15 +336,20 @@
     def send_velocity(phase):
         return lambda side: send_face(side, phase, V, VELOCITY_FACES)
 
-    for which in (far, near, across):
-        at_sides(which, send_stress(0))
-    for load in (loads[1],) + tuple(loads[6:]):
+    for comp, _ in STRESS_FACES[1]:
+        stress_loads.pop(comp).wait()
+    at_sides(far, send_stress(0))
+    at_sides(near, send_stress(0))
+    for load in stress_loads.values():
+        load.wait()
+    at_sides(across, send_stress(0))
+    for load in [loads[0]] + loads[5:]:
         load.wait()
     source_terms()
     for k in range(1, groups):
         source_copy(k).start()
+    loads[1].wait()
     loads[2].wait()
-    loads[3].wait()
     for t in range(steps):
         first, second = 2 * t, 2 * t + 1
         last = t == steps - 1
@@ -342,8 +358,8 @@
             insert_sources(t)
         exchange(first, STRESS_FACES, apply_force, (send_velocity(second),))
         if t == 0:
+            loads[3].wait()
             loads[4].wait()
-            loads[5].wait()
         if t == 0 and last:
             for k in range(1, groups):
                 source_copy(k).wait_recv()
@@ -365,6 +381,18 @@
         finish_faces(2 * t + 1, VELOCITY_FACES)
     for k in range(1, groups):
         source_copy(k).wait_send()
+
+
+def store_kernel(v_ref, s_ref, v_out, s_out, sem):
+    copies = [pltpu.make_async_copy(v_ref, v_out, sem.at[0])]
+    half = s_ref.shape[0] // 2
+    for part in range(2):
+        layers = pl.ds(part * half, half)
+        copies.append(pltpu.make_async_copy(s_ref.at[layers], s_out.at[layers], sem.at[1 + part]))
+    for copy in copies:
+        copy.start()
+    for copy in copies:
+        copy.wait()
 
 
 def local(
@@ -383,7 +411,7 @@
     vmem = pl.BlockSpec(memory_space=pltpu.VMEM)
     dma = pltpu.SemaphoreType.DMA
     phases = 2 * steps
-    return pl.pallas_call(
+    v_last, s_last = pl.pallas_call(
         functools.partial(kernel, groups, blocks, steps),
         out_shape=(
             pltpu.VMEM(velocity.shape, f32),
@@ -406,11 +434,12 @@
             pltpu.VMEM((tall, groups * rows), bf16),
             pltpu.VMEM((cx * cy, groups * rows), bf16),
             pltpu.VMEM((cz, groups * rows), bf16),
-            pltpu.VMEM((phases, 2, 5, cy, cz), f32),
-            pltpu.VMEM((phases, 2, 5, cy, cz), f32),
-            pltpu.VMEM((phases, 2, 5, cx, cz), f32),
-            pltpu.VMEM((phases, 2, 5, cx, cz), f32),
-            dma((10,)),
+            pltpu.VMEM((phases, 2, 9, cy, cz), bf16),
+            pltpu.VMEM((phases, 2, 9, cy, cz), bf16),
+            pltpu.VMEM((phases, 2, 9, cx, cz), bf16),
+            pltpu.VMEM((phases, 2, 9, cx, cz), bf16),
+            dma((6,)),
+            dma((9,)),
             dma((groups,)),
             dma((groups,)),
             dma((phases, 4)),
@@ -420,6 +449,19 @@
     )(
         velocity, stresses, buoyancy, lame_first, rigidity, histories, mechanism.T, resample.T,
         owners.reshape(1, rows), cell_offsets.reshape(1, rows),
+    )
+    return pl.pallas_call(
+        store_kernel,
+        out_shape=(
+            jax.ShapeDtypeStruct(velocity.shape, f32),
+            jax.ShapeDtypeStruct(stresses.shape, f32),
+        ),
+        in_specs=[vmem, vmem],
+        out_specs=(hbm, hbm),
+        scratch_shapes=[dma((3,))],
+    )(
+        pltpu.with_memory_space_constraint(v_last, pltpu.VMEM),
+        pltpu.with_memory_space_constraint(s_last, pltpu.VMEM),
     )
 
 

time: 27.5 us -> 25.6 us (0.931); the launches traced: 27.1 us -> 25.4 us
  local copies, waits for them, and re-layouts: 1.63 us -> 0 us
    unnamed x2 -> x0, local copies, waits for them, and re-layouts: 1.63 us -> none
    pallas_call x0 -> x1, Pallas kernels: none -> 1.03 us  [local(): pl.pallas_call(store_kernel, out_shape=(jax.ShapeDtypeStruct(velocity.sha...]
    pallas_call x1, Pallas kernels: 24.8 us -> 23.8 us  [local(): pl.pallas_call(functools.partial(kernel, groups, blocks, steps), out_shap...]
where the time goes in v3:
time: 25.6 us; the launch traced here: 25.4 us
  Pallas kernels  24.8 us (97%)
  between operations  0.64 us (2%)
    pallas_call x1, Pallas kernels, local(): pl.pallas_call(functools.partial(kernel, groups, blocks, steps), out_shap...  23.8 us
    pallas_call x1, Pallas kernels, local(): pl.pallas_call(store_kernel, out_shape=(jax.ShapeDtypeStruct(velocity.sha...  1.03 us

profile of v3, /device:TPU:0, one launch (start us, length us, event | category | flops | bytes accessed | tf_op | source)
XLA Modules:
  0.0 25.4 jit_solution(12545228165007045780)
XLA Ops:
  0.6 23.8 %shard_map.113 = (f32[3,16,16,128]{3,2,1,0:T(8,128)S(1)}, f32[6,16,16,128]{3,2,1,0:T(8,128)S(1)}) custom-call(f32[3,16,16,128]{3,2,1,0:T(8,128)} %v_hbm.1, f32[6,16,16,128]{3,2,1,0:T(8,128)} %s_hbm.1, f32[16,16,128]{2,1,0:T(8,128)} %buoy_hbm.1, f32[16,16,128]{2,1,0:T(8,128)} %lame_hbm.1, f32[16,16,128]{2,1,0:T(8,128)} %rig_hbm.1, bf16[256,512]{1,0:T(8,128)(2,1)} %hist_hbm.1, ...), custom_call_target="tpu_custom_call" | custom-call | tf_op jit(solution)/shard_map/pallas_call | solution.py:414
  24.4 1.0 %shard_map.114 = (f32[3,16,16,128]{3,2,1,0:T(8,128)}, f32[6,16,16,128]{3,2,1,0:T(8,128)}) custom-call(f32[3,16,16,128]{3,2,1,0:T(8,128)S(1)} %get-tuple-element.4.v_ref, f32[6,16,16,128]{3,2,1,0:T(8,128)S(1)} %get-tuple-element.5.s_ref), custom_call_target="tpu_custom_call" | custom-call | tf_op jit(solution)/shard_map/pallas_call | solution.py:453

commit v4 on v3

--- a/solution.py
+++ b/solution.py
@@ -263,6 +263,16 @@
                 v_out[comp, x] = V[comp, XP + x, pl.ds(YP, cy), :]
         return carry
 
+    def sweep(body):
+        batch = 2 if cx % 2 == 0 else 1
+
+        def several(at, carry):
+            for one in range(batch):
+                carry = body(batch * at + one, carry)
+            return carry
+
+        lax.fori_loop(0, cx // batch, several, 0)
+
     def source_copy(k):
         return pltpu.make_async_remote_copy(
             src_ref=src,
@@ -353,7 +363,7 @@
     for t in range(steps):
         first, second = 2 * t, 2 * t + 1
         last = t == steps - 1
-        lax.fori_loop(0, cx, velocity_inner, 0)
+        sweep(velocity_inner)
         if t > 0:
             insert_sources(t)
         exchange(first, STRESS_FACES, apply_force, (send_velocity(second),))
@@ -365,7 +375,7 @@
                 source_copy(k).wait_recv()
             source_masks()
             insert_sources(0)
-        lax.fori_loop(0, cx, functools.partial(stress_inner, last), 0)
+        sweep(functools.partial(stress_inner, last))
         if t == 0 and not last:
             for k in range(1, groups):
                 source_copy(k).wait_recv()

time: 25.6 us -> 25.5 us (level)
  the two profiles are of different devices: /device:TPU:0 before, /device:TPU:3 now
where the time goes in v4:
time: 25.5 us; the launch traced here: 25.4 us
  Pallas kernels  24.7 us (97%)
  between operations  0.64 us (3%)
    pallas_call x1, Pallas kernels, local(): pl.pallas_call(functools.partial(kernel, groups, blocks, steps), out_shap...  23.7 us
    pallas_call x1, Pallas kernels, local(): pl.pallas_call(store_kernel, out_shape=(jax.ShapeDtypeStruct(velocity.sha...  1.03 us

profile of v4, /device:TPU:3, one launch (start us, length us, event | category | flops | bytes accessed | tf_op | source)
XLA Modules:
  0.0 25.4 jit_solution(13726634854708853077)
XLA Ops:
  0.6 23.7 %shard_map.113 = (f32[3,16,16,128]{3,2,1,0:T(8,128)S(1)}, f32[6,16,16,128]{3,2,1,0:T(8,128)S(1)}) custom-call(f32[3,16,16,128]{3,2,1,0:T(8,128)} %v_hbm.1, f32[6,16,16,128]{3,2,1,0:T(8,128)} %s_hbm.1, f32[16,16,128]{2,1,0:T(8,128)} %buoy_hbm.1, f32[16,16,128]{2,1,0:T(8,128)} %lame_hbm.1, f32[16,16,128]{2,1,0:T(8,128)} %rig_hbm.1, bf16[256,512]{1,0:T(8,128)(2,1)} %hist_hbm.1, ...), custom_call_target="tpu_custom_call" | custom-call | tf_op jit(solution)/shard_map/pallas_call | solution.py:424
  24.4 1.0 %shard_map.114 = (f32[3,16,16,128]{3,2,1,0:T(8,128)}, f32[6,16,16,128]{3,2,1,0:T(8,128)}) custom-call(f32[3,16,16,128]{3,2,1,0:T(8,128)S(1)} %get-tuple-element.4.v_ref, f32[6,16,16,128]{3,2,1,0:T(8,128)S(1)} %get-tuple-element.5.s_ref), custom_call_target="tpu_custom_call" | custom-call | tf_op jit(solution)/shard_map/pallas_call | solution.py:463
